TPU v7x, 32 devices: a whole 2x2x4 slice. The times are simulated.
32 devices in a mesh: grp: 4 (over z), cand: 8 (over y, x, core).
Axes of the slice: x: 2, y: 2, z: 4, core: 2. Of those that a mesh axis runs over, the one named last changes fastest.
Arguments:
- embeddings: bfloat16 [96, 1024, 1024], P('grp', 'cand'), may hold values from -6 to 6
- hidden_weight: bfloat16 [2048, 1024], P('cand'), may hold values from -0.1875 to 0.1875
- score_weight: bfloat16 [2048], replicated, may hold values from -0.5 to 0.5
- relevance: int32 [96, 1024], P('grp', 'cand'), may hold values from 0 to 4
- rank_pos: int32 [96, 1024], P('grp', 'cand'), may hold values from 0 to 1023, as said below
- ideal_dcg: float32 [96], P('grp'), may hold values from 32 to 128
Outputs:
- grad_hidden: float32 [2048, 1024], P('cand')
- lambdas: float32 [96, 1024], P('grp', 'cand')
Inputs may be any that keep to these rules, and one draw needn't show every extreme that they name: `rank_pos`: in each group the rank positions are a permutation of 0 to 1023.
All inputs are finite; a program needn't handle non-finite values.
Results may differ from a plain program's by a relative error of at most 0.006.
Values may be sent and summed in bfloat16 or wider, within the bound.
A program may use at most 64 MiB of HBM per device.

v0:
```python
import jax
import jax.numpy as jnp
from jax import lax
from jax.sharding import PartitionSpec as P

EPS = 1e-06


def pair_lambdas(own_score, own_gain, own_disc, far_score, far_gain, far_disc, ideal):
    gain_diff = far_gain[..., None, :] - own_gain[..., :, None]
    toward = jnp.sign(gain_diff)
    weight = (
        jnp.abs(gain_diff)
        * jnp.abs(far_disc[..., None, :] - own_disc[..., :, None])
        / ideal[..., None, None]
    )
    margin = own_score[..., :, None] - far_score[..., None, :]
    return jnp.sum(weight * toward * jax.nn.sigmoid(toward * margin), axis=-1)


def gain_of(labels):
    return jnp.exp2(labels.astype(jnp.float32)) - 1.0


def discount_of(positions):
    return 1.0 / jnp.log2(2.0 + positions.astype(jnp.float32))


def per_device(embeddings, hidden_weight, score_weight, relevance, rank_pos, ideal_dcg):
    grp_count, local, width = embeddings.shape
    cand_rows = embeddings.reshape(grp_count * local, width)
    pre_act = lax.dot_general(
        cand_rows,
        lax.all_gather(hidden_weight, "cand", axis=0, tiled=True),
        (((1,), (1,)), ((), ())),
        preferred_element_type=jnp.float32,
    )
    acts, pull = jax.vjp(jax.nn.gelu, pre_act)
    scores = jnp.dot(
        acts.astype(jnp.bfloat16), score_weight, preferred_element_type=jnp.float32
    ).reshape(grp_count, local)
    gain_vals = gain_of(relevance)
    discount = discount_of(rank_pos)
    lambdas = pair_lambdas(
        scores,
        gain_vals,
        discount,
        lax.all_gather(scores, "cand", axis=1, tiled=True),
        lax.all_gather(gain_vals, "cand", axis=1, tiled=True),
        lax.all_gather(discount, "cand", axis=1, tiled=True),
        ideal_dcg,
    )
    upstream = (
        lambdas.reshape(grp_count * local)[:, None] * score_weight.astype(jnp.float32)[None, :]
    )
    grad_pre = pull(upstream)[0].astype(jnp.bfloat16)
    owned = lax.psum_scatter(
        lax.dot_general(
            grad_pre, cand_rows, (((0,), (0,)), ((), ())), preferred_element_type=jnp.float32
        ).astype(jnp.bfloat16),
        "cand",
        scatter_dimension=0,
        tiled=True,
    ).astype(jnp.float32)
    summed = lax.psum(owned, "grp")
    squares = lax.psum(jnp.sum(summed * summed), "cand")
    entries = summed.shape[0] * summed.shape[1] * lax.axis_size("cand")
    scale = lax.rsqrt(squares / entries + EPS)
    return (summed * scale, lambdas)


def solution(mesh):
    return jax.shard_map(
        per_device,
        mesh=mesh,
        in_specs=(
            P("grp", "cand", None),
            P("cand", None),
            P(),
            P("grp", "cand"),
            P("grp", "cand"),
            P("grp"),
        ),
        out_specs=(P("cand", None), P("grp", "cand")),
        check_vma=False,
    )
```

profile of v0, /device:TPU:0, one launch (start us, length us, event | category | flops | bytes accessed | tf_op | source)
XLA Modules:
  0.0 254.7 jit_solution(1957202030902142692)
XLA Ops:
  7.2 0.0 all-gather.2.cloned.1.call-start
  7.2 0.7 all-gather.2.cloned.1.call-update
  7.9 0.0 reduce-scatter.2.cloned.1.call-start
  7.9 0.7 reshape.18
  8.6 0.7 convert_element_type.24
  9.3 0.7 exponential_add_fusion
  10.0 10.7 %all_gather.12 = f32[24,1024]{1,0:T(8,128)S(1)} all-gather(f32[24,128]{1,0:T(8,128)S(1)} %exponential_add_fusion), channel_id=1, replica_groups=mesh['grp'=4,'cand'=8] {'cand'}, dimensions={1}, use_global_device_ids=true | all-gather | bytes 110592 | tf_op jit(solution)/shard_map/all_gather | solution.py:49
  20.7 0.7 multiply_divide_fusion
  21.5 9.5 %all_gather.13 = f32[24,1024]{1,0:T(8,128)S(1)} all-gather(f32[24,128]{1,0:T(8,128)S(1)} %multiply_divide_fusion), channel_id=1, replica_groups=mesh['grp'=4,'cand'=8] {'cand'}, dimensions={1}, use_global_device_ids=true | all-gather | bytes 110592 | tf_op jit(solution)/shard_map/all_gather | solution.py:50
  31.0 18.5 %all-gather.2.cloned.1.call-done = bf16[2048,1024]{1,0:T(8,128)(2,1)} async-done(((bf16[256,1024]{1,0:T(8,128)(2,1)}), bf16[2048,1024]{1,0:T(8,128)(2,1)}) %all-gather.2.cloned.1.call-update) | async-done | bytes 4194320 | tf_op jit(solution)/shard_map/all_gather | solution.py:34
  49.5 19.7 %fusion.36 = f32[3072,2048]{1,0:T(8,128)} fusion(bf16[3072,1024]{1,0:T(8,128)(2,1)} %bitcast.11, bf16[2048,1024]{1,0:T(8,128)(2,1)} %all-gather.2.cloned.1.call-done), kind=kOutput, calls=%fused_computation.44 | convolution fusion | flops 12884901888 | bytes 35651584 | tf_op jit(solution)/shard_map/dot_general | solution.py:32
  69.1 0.0 copy-start
  69.1 11.9 %fusion.20 = f32[1,3072]{1,0:T(1,128)S(1)} fusion(bf16[2048,1]{0,1:T(2,128)(2,1)S(1)} %reshape.18, f32[3072,2048]{1,0:T(8,128)} %fusion.36), kind=kOutput, calls=%fused_computation.27 | convolution fusion | flops 69206016 | bytes 25182208 | tf_op jit(solution)/shard_map/dot_general | solution.py:39
  81.1 9.1 %all_gather.15 = f32[24,1024]{1,0:T(8,128)S(1)} all-gather(f32[24,128]{1,0:T(8,128)S(1)} %bitcast.9), channel_id=1, replica_groups=mesh['grp'=4,'cand'=8] {'cand'}, dimensions={1}, use_global_device_ids=true | all-gather | bytes 110592 | tf_op jit(solution)/shard_map/all_gather | solution.py:48
  90.2 0.0 copy-done
  90.2 11.2 %fusion.13 = f32[24,128]{1,0:T(8,128)S(1)} fusion(f32[24,1024]{1,0:T(8,128)S(1)} %all_gather.15, f32[24,128]{1,0:T(8,128)S(1)} %bitcast.10, f32[24]{0:T(128)S(1)} %copy-done, f32[24,128]{1,0:T(8,128)S(1)} %multiply_divide_fusion, f32[24,1024]{1,0:T(8,128)S(1)} %all_gather.13, f32[24,128]{1,0:T(8,128)S(1)} %exponential_add_fusion, f32[24,1024]{1,0:T(8,128)S(1)} %all_gather.12), kind=kLoop, calls=%fused_computation.20 | loop fusion | flops 47182848 | bytes 344160 | tf_op jit(solution)/shard_map/reduce_sum | solution.py:18
  101.4 0.0 copy-start.1
  101.4 35.9 %fusion.23 = bf16[2048,1024]{1,0:T(8,128)(2,1)} fusion(bf16[3072,1024]{1,0:T(8,128)(2,1)} %bitcast.12, f32[3072,2048]{1,0:T(8,128)} %fusion.36, f32[2048]{0:T(1024)S(1)} %convert_element_type.24, f32[3072]{0:T(1024)S(1)} %bitcast.13), kind=kOutput, calls=%fused_computation.29 | convolution fusion | flops 13019119616 | bytes 35672064 | tf_op jit(solution)/shard_map/dot_general | solution.py:58
  137.3 0.0 copy-done.1
  137.3 0.0 reduce-scatter.2.cloned.1.call-update
  137.4 51.3 %reduce-scatter.2.cloned.1.call-done = bf16[256,1024]{1,0:T(8,128)(2,1)} async-done(((bf16[2048,1024]{1,0:T(8,128)(2,1)}), bf16[256,1024]{1,0:T(8,128)(2,1)}) %reduce-scatter.2.cloned.1.call-update) | async-done | bytes 524304 | tf_op jit(solution)/shard_map/reduce_scatter | solution.py:57
  188.7 44.2 %all-reduce.1 = f32[256,1024]{1,0:T(8,128)S(1)} all-reduce(bf16[256,1024]{1,0:T(8,128)(2,1)} %reduce-scatter.2.cloned.1.call-done), channel_id=1, replica_groups=mesh['grp'=4,'cand'=8] {'grp'}, use_global_device_ids=true, to_apply=%region_2.0 | all-reduce | flops 262144 | bytes 1572864 | tf_op jit(solution)/shard_map/psum | solution.py:65
  232.9 0.9 multiply_reduce_fusion
  233.8 12.4 %psum.15 = f32[]{:T(128)} all-reduce(f32[]{:T(128)} %multiply_reduce_fusion), channel_id=1, replica_groups=mesh['grp'=4,'cand'=8] {'cand'}, use_global_device_ids=true, to_apply=%region_4.0 | all-reduce | flops 1 | bytes 8 | tf_op jit(solution)/shard_map/psum | solution.py:66
  246.9 1.0 broadcast_multiply_fusion
Async XLA Ops:
  7.2 42.3 %all-gather.2.cloned.1.call-start = ((), (), s32[]{:S(2)}) async-start(), calls=%async_computation.1 | async-start | bytes 4718592 | tf_op jit(solution)/shard_map/all_gather | solution.py:34
  7.9 180.8 %reduce-scatter.2.cloned.1.call-start = ((), (), s32[]{:S(2)}) async-start(), calls=%async_computation.2 | async-start | bytes 4718592 | tf_op jit(solution)/shard_map/reduce_scatter | solution.py:57
  69.1 21.1 %copy-start = (f32[24]{0:T(128)S(1)}, f32[24]{0:T(128)}, u32[]{:S(2)}) copy-start(f32[24]{0:T(128)} %param.11) | copy-start | bytes 292
  101.4 36.0 %copy-start.1 = (f32[24,128]{1,0:T(8,128)}, f32[24,128]{1,0:T(8,128)S(1)}, u32[]{:S(2)}) copy-start(f32[24,128]{1,0:T(8,128)S(1)} %fusion.13) | copy-start | bytes 36868
Sparse Core Ops, SparseCore 0:
  9.9 39.5 all-gather.1
  137.5 51.1 reduce-scatter.1
where the time goes:
time: 255 us
  blocking collectives  86 us (34%)
  waiting for transfers between devices  70.5 us (28%)
  matrix products  67.5 us (26%)
  other arithmetic  15.2 us (6%)
  between operations  14.8 us (6%)
    reduce_scatter x1, waiting for transfers between devices, per_device(): lax.psum_scatter(lax.dot_general(grad_pre, cand_rows, (((0,), (0,)), ((),...  51.3 us
    psum x1, blocking collectives, per_device(): summed = lax.psum(owned, 'grp')  44.2 us
    dot_general x1, matrix products, per_device(): lax.dot_general(grad_pre, cand_rows, (((0,), (0,)), ((), ())), preferred_...  35.9 us
    dot_general x1, matrix products, per_device(): lax.dot_general(cand_rows, lax.all_gather(hidden_weight, 'cand', axis=0,...  19.7 us
    all_gather x1, waiting for transfers between devices, per_device(): lax.all_gather(hidden_weight, 'cand', axis=0, tiled=True)  18.5 us
    psum x1, blocking collectives, per_device(): squares = lax.psum(jnp.sum(summed * summed), 'cand')  12.4 us
    dot_general x1, matrix products, per_device(): jnp.dot(acts.astype(jnp.bfloat16), score_weight, preferred_element_type=j...  11.9 us
    reduce_sum x1, other arithmetic, pair_lambdas(): return jnp.sum(weight * toward * jax.nn.sigmoid(toward * margin), axis=-1)  11.2 us
  transfers between devices with their start and end apart: 2, of which 2 were waited for; matrix products, arithmetic and copies ran while one was open for 1% of the time, Pallas kernels for 0%

commit v1 on v0

--- a/solution.py
+++ b/solution.py
@@ -62,7 +62,8 @@
         scatter_dimension=0,
         tiled=True,
     ).astype(jnp.float32)
-    summed = lax.psum(owned, "grp")
+    blocks = lax.all_gather(owned, "grp", axis=0, tiled=False)
+    summed = blocks.sum(axis=0)
     squares = lax.psum(jnp.sum(summed * summed), "cand")
     entries = summed.shape[0] * summed.shape[1] * lax.axis_size("cand")
     scale = lax.rsqrt(squares / entries + EPS)

time: 255 us -> 298 us (1.17)
  waiting for transfers between devices: 70.5 us -> 151 us
  blocking collectives: 86 us -> 43.4 us
  other arithmetic: 15.2 us -> 20.1 us
    all_gather x0 -> x1, waiting for transfers between devices: none -> 80.9 us  [per_device(): blocks = lax.all_gather(owned, 'grp', axis=0, tiled=False)]
    psum x1 -> x0, blocking collectives: 44.2 us -> none  [per_device(): summed = lax.psum(owned, 'grp')]
  transfers between devices with their start and end apart: 2 -> 3, of which waited for: 2 -> 3; matrix products, arithmetic and copies ran while one was open for 1% -> 1% of each run, Pallas kernels for 0% -> 0%
where the time goes in v1:
time: 298 us
  waiting for transfers between devices  151 us (51%)
  matrix products  67.5 us (23%)
  blocking collectives  43.4 us (15%)
  other arithmetic  20.1 us (7%)
  between operations  14.5 us (5%)
    all_gather x1, waiting for transfers between devices, per_device(): blocks = lax.all_gather(owned, 'grp', axis=0, tiled=False)  80.9 us
    reduce_scatter x1, waiting for transfers between devices, per_device(): lax.psum_scatter(lax.dot_general(grad_pre, cand_rows, (((0,), (0,)), ((),...  51.3 us
    dot_general x1, matrix products, per_device(): lax.dot_general(grad_pre, cand_rows, (((0,), (0,)), ((), ())), preferred_...  35.9 us
    dot_general x1, matrix products, per_device(): lax.dot_general(cand_rows, lax.all_gather(hidden_weight, 'cand', axis=0,...  19.7 us
    all_gather x1, waiting for transfers between devices, per_device(): lax.all_gather(hidden_weight, 'cand', axis=0, tiled=True)  18.5 us
    psum x1, blocking collectives, per_device(): squares = lax.psum(jnp.sum(summed * summed), 'cand')  14.1 us
    dot_general x1, matrix products, per_device(): jnp.dot(acts.astype(jnp.bfloat16), score_weight, preferred_element_type=j...  11.9 us
    reduce_sum x1, other arithmetic, pair_lambdas(): return jnp.sum(weight * toward * jax.nn.sigmoid(toward * margin), axis=-1)  11.2 us
  transfers between devices with their start and end apart: 3, of which 3 were waited for; matrix products, arithmetic and copies ran while one was open for 1% of the time, Pallas kernels for 0%

profile of v1, /device:TPU:0, one launch (start us, length us, event | category | flops | bytes accessed | tf_op | source)
XLA Modules:
  0.0 297.7 jit_solution(6015672379931126881)
XLA Ops:
  7.2 0.0 all-gather.4.cloned.1.call-start
  7.2 0.7 all-gather.4.cloned.1.call-update
  7.9 0.0 reduce-scatter.2.cloned.1.call-start
  7.9 0.7 reshape.20
  8.6 0.7 convert_element_type.22
  9.3 0.7 exponential_add_fusion
  10.0 10.7 %all_gather.21 = f32[24,1024]{1,0:T(8,128)S(1)} all-gather(f32[24,128]{1,0:T(8,128)S(1)} %exponential_add_fusion), channel_id=1, replica_groups=mesh['grp'=4,'cand'=8] {'cand'}, dimensions={1}, use_global_device_ids=true | all-gather | bytes 110592 | tf_op jit(solution)/shard_map/all_gather | solution.py:49
  20.7 0.7 multiply_divide_fusion
  21.5 9.5 %all_gather.22 = f32[24,1024]{1,0:T(8,128)S(1)} all-gather(f32[24,128]{1,0:T(8,128)S(1)} %multiply_divide_fusion), channel_id=1, replica_groups=mesh['grp'=4,'cand'=8] {'cand'}, dimensions={1}, use_global_device_ids=true | all-gather | bytes 110592 | tf_op jit(solution)/shard_map/all_gather | solution.py:50
  31.0 18.5 %all-gather.4.cloned.1.call-done = bf16[2048,1024]{1,0:T(8,128)(2,1)} async-done(((bf16[256,1024]{1,0:T(8,128)(2,1)}), bf16[2048,1024]{1,0:T(8,128)(2,1)}) %all-gather.4.cloned.1.call-update) | async-done | bytes 4194320 | tf_op jit(solution)/shard_map/all_gather | solution.py:34
  49.5 19.7 %fusion.36 = f32[3072,2048]{1,0:T(8,128)} fusion(bf16[3072,1024]{1,0:T(8,128)(2,1)} %bitcast.13, bf16[2048,1024]{1,0:T(8,128)(2,1)} %all-gather.4.cloned.1.call-done), kind=kOutput, calls=%fused_computation.44 | convolution fusion | flops 12884901888 | bytes 35651584 | tf_op jit(solution)/shard_map/dot_general | solution.py:32
  69.1 0.0 copy-start
  69.1 11.9 %fusion.20 = f32[1,3072]{1,0:T(1,128)S(1)} fusion(bf16[2048,1]{0,1:T(2,128)(2,1)S(1)} %reshape.20, f32[3072,2048]{1,0:T(8,128)} %fusion.36), kind=kOutput, calls=%fused_computation.27 | convolution fusion | flops 69206016 | bytes 25182208 | tf_op jit(solution)/shard_map/dot_general | solution.py:39
  81.1 9.1 %all_gather.24 = f32[24,1024]{1,0:T(8,128)S(1)} all-gather(f32[24,128]{1,0:T(8,128)S(1)} %bitcast.11), channel_id=1, replica_groups=mesh['grp'=4,'cand'=8] {'cand'}, dimensions={1}, use_global_device_ids=true | all-gather | bytes 110592 | tf_op jit(solution)/shard_map/all_gather | solution.py:48
  90.2 0.0 copy-done
  90.2 11.2 %fusion.13 = f32[24,128]{1,0:T(8,128)S(1)} fusion(f32[24,1024]{1,0:T(8,128)S(1)} %all_gather.24, f32[24,128]{1,0:T(8,128)S(1)} %bitcast.12, f32[24]{0:T(128)S(1)} %copy-done, f32[24,128]{1,0:T(8,128)S(1)} %multiply_divide_fusion, f32[24,1024]{1,0:T(8,128)S(1)} %all_gather.22, f32[24,128]{1,0:T(8,128)S(1)} %exponential_add_fusion, f32[24,1024]{1,0:T(8,128)S(1)} %all_gather.21), kind=kLoop, calls=%fused_computation.20 | loop fusion | flops 47182848 | bytes 344160 | tf_op jit(solution)/shard_map/reduce_sum | solution.py:18
  101.4 0.0 copy-start.1
  101.4 35.9 %fusion.23 = bf16[2048,1024]{1,0:T(8,128)(2,1)} fusion(bf16[3072,1024]{1,0:T(8,128)(2,1)} %bitcast.14, f32[3072,2048]{1,0:T(8,128)} %fusion.36, f32[2048]{0:T(1024)S(1)} %convert_element_type.22, f32[3072]{0:T(1024)S(1)} %bitcast.15), kind=kOutput, calls=%fused_computation.29 | convolution fusion | flops 13019119616 | bytes 35672064 | tf_op jit(solution)/shard_map/dot_general | solution.py:58
  137.4 0.0 copy-done.1
  137.4 0.0 reduce-scatter.2.cloned.1.call-update
  137.4 0.0 all-gather.6.cloned.1.call-start
  137.5 51.3 %reduce-scatter.2.cloned.1.call-done = bf16[256,1024]{1,0:T(8,128)(2,1)} async-done(((bf16[2048,1024]{1,0:T(8,128)(2,1)}), bf16[256,1024]{1,0:T(8,128)(2,1)}) %reduce-scatter.2.cloned.1.call-update) | async-done | bytes 524304 | tf_op jit(solution)/shard_map/reduce_scatter | solution.py:57
  188.7 2.1 all_gather.28
  190.9 0.0 all-gather.6.cloned.1.call-update
  190.9 80.9 %all-gather.6.cloned.1.call-done = f32[1024,1024]{1,0:T(8,128)} async-done(((f32[256,1024]{1,0:T(8,128)}), f32[1024,1024]{1,0:T(8,128)}) %all-gather.6.cloned.1.call-update) | async-done | bytes 4194320 | tf_op jit(solution)/shard_map/all_gather | solution.py:65
  271.8 2.7 reduce_sum.28
  274.5 0.9 multiply_reduce_fusion
  275.4 14.1 %psum.7 = f32[]{:T(128)} all-reduce(f32[]{:T(128)} %multiply_reduce_fusion), channel_id=1, replica_groups=mesh['grp'=4,'cand'=8] {'cand'}, use_global_device_ids=true, to_apply=%region_4.0 | all-reduce | flops 1 | bytes 8 | tf_op jit(solution)/shard_map/psum | solution.py:67
  290.1 1.0 broadcast_multiply_fusion
Async XLA Ops:
  7.2 42.3 %all-gather.4.cloned.1.call-start = ((), (), s32[]{:S(2)}) async-start(), calls=%async_computation.1 | async-start | bytes 4718592 | tf_op jit(solution)/shard_map/all_gather | solution.py:34
  7.9 180.8 %reduce-scatter.2.cloned.1.call-start = ((), (), s32[]{:S(2)}) async-start(), calls=%async_computation.2 | async-start | bytes 4718592 | tf_op jit(solution)/shard_map/reduce_scatter | solution.py:57
  69.1 21.1 %copy-start = (f32[24]{0:T(128)S(1)}, f32[24]{0:T(128)}, u32[]{:S(2)}) copy-start(f32[24]{0:T(128)} %param.11) | copy-start | bytes 292
  101.4 36.0 %copy-start.1 = (f32[24,128]{1,0:T(8,128)}, f32[24,128]{1,0:T(8,128)S(1)}, u32[]{:S(2)}) copy-start(f32[24,128]{1,0:T(8,128)S(1)} %fusion.13) | copy-start | bytes 36868
  137.4 134.4 %all-gather.6.cloned.1.call-start = ((), (), s32[]{:S(2)}) async-start(), calls=%async_computation.3 | async-start | bytes 5242880 | tf_op jit(solution)/shard_map/all_gather | solution.py:65
Sparse Core Ops, SparseCore 0:
  9.9 39.5 all-gather.3
  137.5 51.1 reduce-scatter.1
  191.0 80.7 all-gather.5
